TPU v7x, 32 devices: a whole 2x2x4 slice. The times are simulated.
32 devices in a mesh: box: 4 (over z), tile: 8 (over y, x, core).
Axes of the slice: x: 2, y: 2, z: 4, core: 2. Of those that a mesh axis runs over, the one named last changes fastest.
Arguments:
- box_maps: float32 [4, 6, 448, 2688], P('box', None, 'tile'), may hold values from -4.01 to 4.01, as said below
- face_slots: int32 [4, 6], replicated, may hold values from 0 to 5, each once within a row
Outputs:
- final_map: float32 [7168, 7168], P('tile', 'box')
Inputs may be any that keep to these rules, and one draw needn't show every extreme that they name: `box_maps`: read as a matrix of order 6 * 448 with rows and columns ordered by stored block and node, each box's map is exactly symmetric and positive definite. `face_slots`: each row is a permutation of the six stored blocks.
All inputs are finite; a program needn't handle non-finite values.
Results may differ from a plain program's by a relative error of at most 0.0001.
Values sent between devices are 32-bit elements; how exact they have to be, the bound alone decides.
A program may use at most 128 MiB of HBM per device.

v0:
```python
import jax
import jax.numpy as jnp
from jax import lax
from jax.experimental import pallas as pl
from jax.experimental.pallas import tpu as pltpu
from jax.sharding import PartitionSpec as P

MESH = pl.DeviceIdType.MESH
HIGHEST = lax.Precision.HIGHEST
HIGH = lax.Precision.HIGH
BLOCK = 64
LANES = 128


def dot(left, right, precision=HIGHEST):
    return jnp.dot(left, right, precision=precision, preferred_element_type=jnp.float32)


def dot_nt(left, right, precision=HIGHEST):
    return lax.dot_general(
        left, right, (((1,), (1,)), ((), ())), precision=precision, preferred_element_type=jnp.float32
    )


def face_order(box_id):
    along_x, along_y = box_id % 2, box_id // 2
    return 1 - along_x, (along_x, 2 + along_y, 4, 5), 3 - along_y


def pick_kernel(slots_ref, stored_ref, shared_ref, rows_ref, own_ref):
    size = shared_ref.shape[-1]
    box_id = lax.axis_index("box")
    x_face, final_faces, y_face = face_order(box_id)
    slot_of = [slots_ref[box_id, face] for face in (x_face, y_face) + final_faces]
    width = -(-(size + BLOCK) // LANES) * LANES

    def piece(row_slot, col_slot):
        start = col_slot * size
        low = start // LANES * LANES
        window = stored_ref[row_slot, :, pl.ds(pl.multiple_of(low, LANES), width)]
        return jnp.where(start == low, window[:, :size], window[:, BLOCK : BLOCK + size])

    x_slot, y_slot, *finals = slot_of
    shared_ref[0] = piece(x_slot, x_slot)
    shared_ref[1] = piece(y_slot, x_slot)
    shared_ref[2] = piece(y_slot, y_slot)
    for index, row_slot in enumerate(finals):
        rows_ref[index] = jnp.concatenate([piece(row_slot, x_slot), piece(row_slot, y_slot)], 1)
        own_ref[index] = jnp.concatenate([piece(row_slot, col_slot) for col_slot in finals], 1)


def pick_faces(stored, face_slots):
    _, nodes, extent = stored.shape
    size = extent // 6
    return pl.pallas_call(
        pick_kernel,
        out_shape=[
            jax.ShapeDtypeStruct((3, nodes, size), jnp.float32),
            jax.ShapeDtypeStruct((4, nodes, 2 * size), jnp.float32),
            jax.ShapeDtypeStruct((4, nodes, 4 * size), jnp.float32),
        ],
        in_specs=[pl.BlockSpec(memory_space=pltpu.SMEM), pl.BlockSpec(memory_space=pltpu.VMEM)],
        out_specs=[pl.BlockSpec(memory_space=pltpu.VMEM)] * 3,
        name="pick_faces",
    )(face_slots, stored)


def leaf_inverse(work_ref):
    size = work_ref.shape[0]

    def octet(index, carry):
        base = pl.multiple_of(index * 8, 8)
        whole = work_ref[...]
        panel = work_ref[pl.ds(base, 8), :]
        lanes = lax.broadcasted_iota(jnp.int32, whole.shape, 1)
        rows = lax.broadcasted_iota(jnp.int32, whole.shape, 0)
        panel_lanes = lax.broadcasted_iota(jnp.int32, panel.shape, 1)
        panel_rows = lax.broadcasted_iota(jnp.int32, panel.shape, 0)
        cols = [
            jnp.broadcast_to(jnp.sum(jnp.where(lanes == base + j, whole, 0.0), 1, keepdims=True), whole.shape)
            for j in range(8)
        ]
        pivots = [
            jnp.broadcast_to(
                jnp.sum(jnp.where(panel_lanes == base + j, panel, 0.0), 1, keepdims=True), panel.shape
            )
            for j in range(8)
        ]
        change = jnp.zeros_like(whole)
        for j in range(8):
            inverse = 1.0 / pivots[j][j : j + 1]
            others = jnp.where(panel_rows != j, pivots[j] * inverse, 0.0)
            scaled = cols[j] * inverse
            for k in range(j + 1, 8):
                head = pivots[k][j : j + 1]
                pivots[k] = pivots[k] - others * head
                cols[k] = cols[k] - scaled * head
            row = panel[j : j + 1]
            change = change + scaled * row
            panel = panel - others * row
        inside = jnp.logical_and(rows >= base, rows < base + 8)
        work_ref[...] = jnp.where(inside, whole, whole - change)
        work_ref[pl.ds(base, 8), :] = panel
        return carry

    lax.fori_loop(0, size // 8, octet, 0)
    done = work_ref[...]
    lanes = lax.broadcasted_iota(jnp.int32, done.shape, 1)
    rows = lax.broadcasted_iota(jnp.int32, done.shape, 0)
    diagonal = jnp.sum(jnp.where(lanes == rows, done, 0.0), 1, keepdims=True)
    return done[:, size:] * (1.0 / diagonal)


def invert(ref, work_ref, between):
    order = ref.shape[0]
    row_ids = lax.broadcasted_iota(jnp.int32, (BLOCK, BLOCK), 0)
    col_ids = lax.broadcasted_iota(jnp.int32, (BLOCK, BLOCK), 1)
    eye = jnp.where(row_ids == col_ids, 1.0, 0.0).astype(jnp.float32)
    for start in range(0, order, BLOCK):
        stop = start + BLOCK
        work_ref[...] = jnp.concatenate([ref[start:stop, start:stop], eye], 1)
        inverse = leaf_inverse(work_ref)
        left = ref[:, start:stop]
        ids = lax.broadcasted_iota(jnp.int32, left.shape, 0)
        left = jnp.where(jnp.logical_and(ids >= start, ids < stop), 0.0, left)
        ref[:, start:stop] = jnp.zeros((order, BLOCK), jnp.float32)
        ref[start:stop, start:stop] = eye
        panel = dot(inverse, ref[start:stop, :])
        ref[start:stop, :] = panel
        ref[...] -= dot(left, panel)
        between(start // BLOCK)


def merge_kernel(
    tiles,
    shared_ref,
    rows_ref,
    own_ref,
    left_ref,
    wide_ref,
    exact_ref,
    z_ref,
    sum_ref,
    part_ref,
    beta_ref,
    pack_ref,
    both_ref,
    far_ref,
    inv_ref,
    couple_ref,
    half_ref,
    other_ref,
    full_ref,
    link_ref,
    temp_ref,
    work_ref,
    middle_ref,
    tall_ref,
    relay_ref,
    z_sems,
    part_sems,
    far_sems,
    line_sems,
    cross_sems,
    twin_sems,
    tall_sems,
    exact_sems,
    relay_sems,
    swap_sems,
    local_sems,
):
    size = shared_ref.shape[-1]
    nodes = shared_ref.shape[1]
    boxes = beta_ref.shape[0]
    slots = tall_ref.shape[0]
    wide_cols, wide_rows = cross_sems.shape[2] + 1, cross_sems.shape[3] + 1
    relays = wide_cols == 2 and wide_rows == 2 and tiles == 2 * boxes
    box_id = lax.axis_index("box")
    tile_id = lax.axis_index("tile")
    core = tile_id % 2
    twin = tile_id + 1 - 2 * core
    own_pair = box_id // 2
    mate = box_id + 1 - 2 * (box_id % 2)
    across = (box_id + 2) % boxes
    chip = tile_id // 2
    row, col = chip // wide_cols, chip % wide_cols

    def tile_at(down, right, on=core):
        return (((row + down + wide_rows) % wide_rows) * wide_cols + (col + right + wide_cols) % wide_cols) * 2 + on

    def remote(source, target, sems, index, box, tile):
        return pltpu.make_async_remote_copy(
            src_ref=source,
            dst_ref=target,
            send_sem=sems.at[(0,) + index],
            recv_sem=sems.at[(1,) + index],
            device_id={"box": box, "tile": tile},
            device_id_type=MESH,
        )

    def each(low, high, action):
        def step(index, carry):
            action(index)
            return carry

        lax.fori_loop(low, high, step, 0)

    barrier = pltpu.get_barrier_semaphore()

    def greet(box, tile):
        pl.semaphore_signal(barrier, inc=1, device_id={"box": box, "tile": tile}, device_id_type=MESH)

    each(1, boxes, lambda i: greet((box_id + i) % boxes, tile_id))
    each(1, tiles, lambda i: greet(box_id, (tile_id + i) % tiles))
    pl.semaphore_wait(barrier, boxes + tiles - 2)

    def chain_step(own, buffer, sems, base, step, sends, action):
        for side, shift in ((0, 1), (1, -1)):
            target = box_id + shift
            origin = box_id - shift * (step - 1) if sends else box_id - shift * step
            valid = jnp.logical_and(origin >= 0, origin < boxes)
            if sends:
                valid = jnp.logical_and(valid, jnp.logical_and(target >= 0, target < boxes))

            @pl.when(valid)
            def _():
                source = own if step == 1 and sends else buffer.at[origin]
                neighbour = (target + boxes) % boxes
                copy = remote(source, buffer.at[origin], sems, (base + side, step - 1), neighbour, tile_id)
                action(copy, origin)

    def start(copy, *rest):
        copy.start()

    def sent(copy, *rest):
        copy.wait_send()

    def came(copy, *rest):
        copy.wait_recv()

    def mate_copy():
        return remote(shared_ref.at[0], z_ref.at[0], z_sems, (0, 0), mate, tile_id)

    def across_copy(pair):
        return remote(sum_ref.at[pair, 0], sum_ref.at[pair, 0], z_sems, (0, 1), across, tile_id)

    def side_copy():
        return remote(shared_ref.at[2], z_ref.at[1], z_sems, (0, 2), across, tile_id)

    def back_copy(side):
        return remote(sum_ref.at[side, 1], sum_ref.at[side, 1], z_sems, (3, 0), mate, tile_id)

    def link_step(step, sends, action):
        chain_step(shared_ref.at[1], beta_ref, z_sems, 1, step, sends, action)

    def part_copy(kind, i, sender):
        tile = (tile_id + i) % tiles
        pair = tile % 2
        if kind == 1:
            source, target = pack_ref.at[pair], both_ref.at[sender]
        else:
            source, target = sum_ref.at[pair, kind // 2], part_ref.at[kind // 2, sender]
        return remote(source, target, part_sems, (kind, i - 1), box_id, tile)

    def part_start(kind, pair):
        def one(i):
            @pl.when((tile_id + i) % 2 == pair)
            def _():
                part_copy(kind, i, tile_id).start()

        each(1, tiles, one)

    def pack(pair):
        pack_ref[pair, :, :size] = beta_ref[2 * pair]
        pack_ref[pair, :, size:] = beta_ref[2 * pair + 1]
        part_start(1, pair)

    mate_copy().start()
    link_step(1, True, start)
    side_copy().start()
    beta_ref[box_id] = shared_ref[1]
    mate_copy().wait_recv()
    sum_ref[own_pair, 0] = shared_ref[0] + z_ref[0]
    across_copy(own_pair).start()
    part_start(0, own_pair)
    link_step(1, False, came)
    link_step(2, True, start)
    pack(own_pair)
    across_copy(1 - own_pair).wait_recv()
    part_start(0, 1 - own_pair)
    side_copy().wait_recv()
    own_side = box_id % 2
    sum_ref[own_side, 1] = shared_ref[2] + z_ref[1]
    back_copy(own_side).start()
    part_start(2, own_side)
    link_step(2, False, came)
    link_step(3, True, start)
    link_step(3, False, came)
    pack(1 - own_pair)
    back_copy(1 - own_side).wait_recv()
    part_start(2, 1 - own_side)
    part_ref[0, tile_id] = sum_ref[core, 0]
    part_ref[1, tile_id] = sum_ref[core, 1]
    both_ref[tile_id] = pack_ref[core]

    def far_step(step, sends, action):
        chain_step(rows_ref, far_ref, far_sems, 0, step, sends, action)

    far_step(1, True, start)

    def line_copy(axis, i, sender):
        dest = tile_at(0, i) if axis == 0 else tile_at(i, 0)
        return remote(rows_ref, wide_ref.at[:, sender], line_sems, (axis, i - 1), box_id, dest)

    def line_source(axis, i):
        return tile_at(0, -i) if axis == 0 else tile_at(-i, 0)

    def cross_copy(axis, i, j, sender):
        dest = tile_at(j, 0) if axis == 0 else tile_at(0, i)
        part = wide_ref.at[pl.ds(2 * axis, 2), sender]
        return remote(part, part, cross_sems, (axis, i - 1, j - 1), box_id, dest)

    def twin_copy(i, j, on):
        sender = tile_at(-j, -i, on)
        source = rows_ref if isinstance(i, int) and isinstance(j, int) else wide_ref.at[:, sender]
        return remote(source, wide_ref.at[:, sender], twin_sems, (i, j), box_id, twin)

    each(1, wide_cols, lambda i: line_copy(0, i, tile_id).start())
    each(1, wide_rows, lambda j: line_copy(1, j, tile_id).start())
    twin_copy(0, 0, core).start()
    keep = pltpu.make_async_copy(rows_ref, wide_ref.at[:, tile_id], local_sems.at[0])
    keep.start()

    def owner(box, face, tile):
        flat = (box * 4 + face) * tiles + tile
        return flat // slots, flat % slots

    def exact_move(face, remote_action, local_action):
        dest, slot = owner(box_id, face, tile_id)
        direct = dest != tile_id

        @pl.when(dest == tile_id)
        def _():
            local_action(
                pltpu.make_async_copy(own_ref.at[face], exact_ref.at[slot], local_sems.at[1 + face])
            )

        if relays:
            dest_row, dest_col = dest // 2 // wide_cols, dest // 2 % wide_cols
            corner = jnp.logical_and(dest_row != row, dest_col != col)
            direct = jnp.logical_and(direct, jnp.logical_not(corner))
            via = tile_at(0, 1) if face % 2 == 0 else tile_at(1, 0)

            @pl.when(corner)
            def _():
                remote_action(
                    pltpu.make_async_remote_copy(
                        src_ref=own_ref.at[face],
                        dst_ref=relay_ref.at[face // 2],
                        send_sem=exact_sems.at[0, face],
                        recv_sem=relay_sems.at[1, face // 2],
                        device_id={"box": box_id, "tile": via},
                        device_id_type=MESH,
                    )
                )

        @pl.when(direct)
        def _():
            remote_action(
                pltpu.make_async_remote_copy(
                    src_ref=own_ref.at[face],
                    dst_ref=exact_ref.at[slot],
                    send_sem=exact_sems.at[0, face],
                    recv_sem=exact_sems.at[1, slot],
                    device_id={"box": box_id, "tile": dest},
                    device_id_type=MESH,
                )
            )

    def relay_move(half, starting):
        dest_chip = owner(box_id, 0, 0)[0] // 2
        dest_row, dest_col = dest_chip // wide_cols, dest_chip % wide_cols

        def one(face, origin):
            dest, slot = owner(box_id, face, origin)
            copy = pltpu.make_async_remote_copy(
                src_ref=relay_ref.at[half],
                dst_ref=exact_ref.at[slot],
                send_sem=relay_sems.at[0, half],
                recv_sem=exact_sems.at[1, slot],
                device_id={"box": box_id, "tile": dest},
                device_id_type=MESH,
            )
            if starting:
                remote(own_ref.at[face], relay_ref.at[half], relay_sems, (half,), box_id, origin).wait_recv()
                copy.start()
            else:
                copy.wait_send()

        @pl.when(jnp.logical_and(col == dest_col, row != dest_row))
        def _():
            one(2 * half, tile_at(0, 1))

        @pl.when(jnp.logical_and(row == dest_row, col != dest_col))
        def _():
            one(2 * half + 1, tile_at(1, 0))

    def tall_move(box, face, starting):
        dest, slot = owner(box, face, tile_id)

        @pl.when(dest == tile_id)
        def _():
            if starting:
                tall_ref[slot] = far_ref[box, face]

        @pl.when(dest != tile_id)
        def _():
            copy = pltpu.make_async_remote_copy(
                src_ref=far_ref.at[box, face],
                dst_ref=tall_ref.at[slot],
                send_sem=tall_sems.at[0, 4 * box + face],
                recv_sem=tall_sems.at[1, slot],
                device_id={"box": box_id, "tile": dest},
                device_id_type=MESH,
            )
            if starting:
                copy.start()
            else:
                copy.wait_send()

    for face in range(4):
        exact_move(face, start, start)

    def spread(step, starting):
        for origin in (box_id - step, box_id + step):

            @pl.when(jnp.logical_and(origin >= 0, origin < boxes))
            def _():
                for face in range(4):
                    tall_move(origin, face, starting)

    def forward_far(step):
        far_step(step, False, came)
        if step < boxes - 1:
            far_step(step + 1, True, start)

        spread(step, True)

    def forward_row(i):
        line_copy(0, i, line_source(0, i)).wait_recv()
        each(1, wide_rows, lambda j: cross_copy(0, i, j, line_source(0, i)).start())
        twin_copy(i, 0, core).start()

    def forward_col(j):
        line_copy(1, j, line_source(1, j)).wait_recv()
        each(1, wide_cols, lambda i: cross_copy(1, i, j, line_source(1, j)).start())
        twin_copy(0 * j, j, core).start()

    def cross_cell(i, j):
        sender = tile_at(-j, -i)
        cross_copy(0, i, j, sender).wait_recv()
        cross_copy(1, i, j, sender).wait_recv()
        twin_copy(i, j, core).start()

    def forward_cross():
        each(1, wide_cols, lambda i: each(1, wide_rows, lambda j: cross_cell(i, j)))

    def forward_line():
        each(1, wide_cols, forward_row)
        each(1, wide_rows, forward_col)

    def forward_relay():
        if relays:
            for half in range(2):
                relay_move(half, True)

    def part_wait(kind):
        each(1, tiles, lambda i: part_copy(kind, i, (tile_id + tiles - i) % tiles).wait_recv())

    def matrix(ref, span):
        if nodes % 8 == 0:
            return ref[...].reshape(tiles * nodes, span)
        for tile in range(tiles):
            middle_ref[tile * nodes : (tile + 1) * nodes, :span] = ref[tile]
        return middle_ref[:size, :span]

    def swap(ref, index):
        return remote(ref, ref, swap_sems, (index,), box_id, twin)

    def half_swap(index):
        return remote(half_ref.at[index], other_ref.at[index], swap_sems, (2 + index,), box_id, twin)

    hooks = {
        (1, 0): lambda: forward_far(1),
        (1, 2): forward_line,
        (1, 5): lambda: forward_far(2),
        (2, 0): forward_cross,
        (2, 2): forward_relay,
        (2, 4): lambda: forward_far(3),
    }

    def stage(index, carry):
        @pl.when(index == 0)
        def _():
            part_wait(0)
            temp_ref[...] = matrix(part_ref.at[0], size)

        @pl.when(index == 1)
        def _():
            inv_ref[core] = temp_ref[...]
            swap(inv_ref.at[core], 0).start()
            part_wait(1)
            linked = matrix(both_ref, 2 * size)
            for side in range(2):
                link_ref[side] = linked[:, side * size : (side + 1) * size]

            def couple(side):
                couple_ref[core, side] = dot(link_ref[side], inv_ref[core])

            each(0, 2, couple)
            swap(couple_ref.at[core], 1).start()
            part_wait(2)
            shared = matrix(part_ref.at[1], size)
            temp_ref[...] = shared

            def term(item):
                side, other = item // 2, (item + 1) // 2
                own = jnp.logical_and(side == other, side == core)
                direct = jnp.where(own, temp_ref[...], 0.0)
                half_ref[item] = direct - dot_nt(couple_ref[core, side], link_ref[other])
                half_swap(item).start()

            each(0, 3, term)
            half_swap(0).wait_recv()
            temp_ref[...] = half_ref[0] + other_ref[0]

        @pl.when(index == 2)
        def _():
            full_ref[0, 0] = temp_ref[...]
            half_swap(1).wait_recv()
            cross = half_ref[1] + other_ref[1]
            link_ref[0] = dot(full_ref[0, 0], cross)
            half_swap(2).wait_recv()
            temp_ref[...] = half_ref[2] + other_ref[2] - dot(cross.T, link_ref[0])

        def between(block):
            for (when, at), action in hooks.items():
                if at == block:
                    pl.when(index == when)(action)

        invert(temp_ref, work_ref, between)
        return carry

    lax.fori_loop(0, 3, stage, 0)
    full_ref[1, 1] = temp_ref[...]
    temp_ref[...] = link_ref[0]
    full_ref[0, 1] = -dot(temp_ref[...], full_ref[1, 1])
    full_ref[1, 0] = full_ref[0, 1].T
    full_ref[0, 0] = full_ref[0, 0] - dot_nt(full_ref[0, 1], temp_ref[...])
    swap(inv_ref.at[1 - core], 0).wait_recv()
    swap(couple_ref.at[1 - core], 1).wait_recv()
    row_box = tile_id * boxes // tiles
    row_pair, row_side = row_box // 2, row_box % 2
    col_pair, col_side = box_id // 2, box_id % 2

    def spread_inverse(item):
        side = jnp.where(item == 2, col_side, item)
        pair = jnp.where(item == 2, row_pair, col_pair)
        link_ref[item] = dot(full_ref[side, 0], couple_ref[pair, 0], HIGH) + dot(
            full_ref[side, 1], couple_ref[pair, 1], HIGH
        )

    each(0, 3, spread_inverse)
    middle_ref[:size, size:] = -link_ref[2].T
    middle_ref[size:, :size] = -link_ref[row_side]
    middle_ref[size:, size:] = full_ref[row_side, col_side]
    corner = dot(couple_ref[row_pair, 0].T, link_ref[0], HIGH) + dot(
        couple_ref[row_pair, 1].T, link_ref[1], HIGH
    )
    middle_ref[:size, :size] = corner + jnp.where(row_pair == col_pair, inv_ref[row_pair], 0.0)

    def twin_wait(i, j):
        twin_copy(i, j, 1 - core).wait_recv()

    each(0, wide_cols, lambda i: each(0, wide_rows, lambda j: twin_wait(i, j)))
    keep.wait()

    def slot_copy(slot):
        flat = tile_id * slots + slot
        source = wide_ref.at[flat // tiles % 4, flat % tiles]
        return pltpu.make_async_copy(source, tall_ref.at[slot], local_sems.at[5 + slot])

    @pl.when(row_box == box_id)
    def _():
        each(0, slots, lambda slot: slot_copy(slot).start())
        each(0, slots, lambda slot: slot_copy(slot).wait())

    def slot_wait(slot):
        source = (tile_id * slots + slot) % tiles

        @pl.when(jnp.logical_and(source != tile_id, row_box != box_id))
        def _():
            remote(rows_ref.at[0], tall_ref.at[slot], tall_sems, (slot,), box_id, twin).wait_recv()

    each(0, slots, slot_wait)
    if nodes % 8 == 0:
        step = slots // 2

        def product(index, carry):
            piece = tall_ref[pl.ds(index * step, step)].reshape(step * nodes, 2 * size)
            rows = pl.ds(pl.multiple_of(index * step * nodes, 8), step * nodes)
            left_ref[rows, :] = dot(piece, middle_ref[...], HIGH)
            return carry

        lax.fori_loop(0, 2, product, 0)
    else:
        for slot in range(slots):
            left_ref[slot * nodes : (slot + 1) * nodes, :] = tall_ref[slot]
        left_ref[...] = dot(left_ref[...], middle_ref[...], HIGH)

    def exact_wait(slot):
        source = (tile_id * slots + slot) % tiles

        @pl.when(jnp.logical_and(source != tile_id, row_box == box_id))
        def _():
            remote(own_ref.at[0], exact_ref.at[slot], exact_sems, (slot,), box_id, twin).wait_recv()

    each(0, slots, exact_wait)

    for face in range(4):
        exact_move(face, sent, lambda copy: copy.wait())
    if relays:
        for half in range(2):
            relay_move(half, False)
    for step in range(1, boxes):
        far_step(step, True, sent)
        link_step(step, True, sent)
        spread(step, False)
    mate_copy().wait_send()
    across_copy(own_pair).wait_send()
    side_copy().wait_send()
    back_copy(own_side).wait_send()
    for kind in range(3):
        each(1, tiles, lambda i: part_copy(kind, i, tile_id).wait_send())
    each(1, wide_cols, lambda i: line_copy(0, i, tile_id).wait_send())
    each(1, wide_rows, lambda j: line_copy(1, j, tile_id).wait_send())

    def cross_sent(i, j):
        cross_copy(0, i, j, line_source(0, i)).wait_send()
        cross_copy(1, i, j, line_source(1, j)).wait_send()

    each(1, wide_cols, lambda i: each(1, wide_rows, lambda j: cross_sent(i, j)))
    each(0, wide_cols, lambda i: each(0, wide_rows, lambda j: twin_copy(i, j, core).wait_send()))
    swap(inv_ref.at[core], 0).wait_send()
    swap(couple_ref.at[core], 1).wait_send()
    for index in range(3):
        half_swap(index).wait_send()


def merge(shared, rows, own):
    _, nodes, size = shared.shape
    tiles, boxes = lax.axis_size("tile"), lax.axis_size("box")
    slots = 4 * boxes
    square = (size, size)
    wide_cols = 1 << ((tiles // 2).bit_length() - 1) // 2
    wide_rows = tiles // 2 // wide_cols

    def vmem(*shape):
        return pltpu.VMEM(shape, jnp.float32)

    def sems(*shape):
        return pltpu.SemaphoreType.DMA((2,) + shape)

    def kernel(*refs):
        merge_kernel(tiles, *refs)

    return pl.pallas_call(
        kernel,
        out_shape=[
            jax.ShapeDtypeStruct((slots * nodes, 2 * size), jnp.float32),
            jax.ShapeDtypeStruct((4, tiles, nodes, 2 * size), jnp.float32),
            jax.ShapeDtypeStruct((slots, nodes, 4 * size), jnp.float32),
        ],
        in_specs=[pl.BlockSpec(memory_space=pltpu.VMEM)] * 3,
        out_specs=[pl.BlockSpec(memory_space=pltpu.VMEM)] + [pl.BlockSpec(memory_space=pltpu.HBM)] * 2,
        scratch_shapes=[
            vmem(2, nodes, size),
            vmem(2, 2, nodes, size),
            vmem(2, tiles, nodes, size),
            vmem(boxes, nodes, size),
            vmem(2, nodes, 2 * size),
            vmem(tiles, nodes, 2 * size),
            vmem(boxes, 4, nodes, 2 * size),
            vmem(2, *square),
            vmem(2, 2, *square),
            vmem(3, *square),
            vmem(3, *square),
            vmem(2, 2, *square),
            vmem(3, *square),
            vmem(*square),
            vmem(BLOCK, 2 * BLOCK),
            vmem(2 * size, 2 * size),
            vmem(slots, nodes, 2 * size),
            vmem(2, nodes, 4 * size),
            sems(4, boxes - 1),
            sems(3, tiles - 1),
            sems(2, boxes - 1),
            sems(2, max(wide_cols, wide_rows)),
            sems(2, wide_cols - 1, wide_rows - 1),
            sems(wide_cols, wide_rows),
            sems(slots),
            sems(slots),
            sems(2),
            sems(5),
            pltpu.SemaphoreType.DMA((5 + slots,)),
        ],
        compiler_params=pltpu.CompilerParams(
            collective_id=0, has_side_effects=True, vmem_limit_bytes=60 * 2**20
        ),
        name="merge",
    )(shared, rows, own)


def per_device(box_maps, face_slots):
    shared, rows, own = pick_faces(box_maps[0], face_slots)
    _, nodes, size = shared.shape
    left, wide, exact = merge(shared, rows, own)
    tiles, boxes = lax.axis_size("tile"), lax.axis_size("box")
    box_id, tile_id = lax.axis_index("box"), lax.axis_index("tile")
    same = tile_id * boxes // tiles == box_id
    exact = jnp.where(same, exact.reshape(left.shape[0], 4 * size), 0.0)
    return exact - dot_nt(left, wide.reshape(4 * tiles * nodes, 2 * size), HIGH)


def solution(mesh):
    return jax.shard_map(
        per_device,
        mesh=mesh,
        in_specs=(P("box", None, "tile", None), P()),
        out_specs=P("tile", "box"),
        check_vma=False,
    )
```

profile of v0, /device:TPU:7, one launch (start us, length us, event | category | flops | bytes accessed | tf_op | source)
XLA Modules:
  0.0 188.1 jit_solution(7743982048265559626)
XLA Ops:
  0.0 4.8 %pick_faces.1 = (f32[3,56,448]{2,1,0:T(8,128)}, f32[4,56,896]{2,1,0:T(8,128)}, f32[4,56,1792]{2,1,0:T(8,128)}) custom-call(s32[4,6]{1,0:T(4,128)} %slots_ref.1, f32[6,56,2688]{2,1,0:T(8,128)} %bitcast.7), custom_call_target="tpu_custom_call" | custom-call | tf_op jit(solution)/shard_map/pick_faces/pallas_call | solution.py:55
  4.8 167.2 %merge.1 = (f32[896,896]{1,0:T(8,128)}, f32[4,8,56,896]{3,2,1,0:T(8,128)}, f32[16,56,1792]{2,1,0:T(8,128)}) custom-call(f32[3,56,448]{2,1,0:T(8,128)} %get-tuple-element.11.refs_0_, f32[4,56,896]{2,1,0:T(8,128)} %get-tuple-element.12.refs_1_, f32[4,56,1792]{2,1,0:T(8,128)} %get-tuple-element.13.refs_2_), custom_call_target="tpu_custom_call" | custom-call | tf_op jit(solution)/shard_map/merge/pallas_call | solution.py:677
  172.0 0.0 copy-start
  172.0 0.0 copy-start.1
  172.1 0.5 broadcast_select_fusion
  172.6 2.3 %copy-done = f32[4,8,56,896]{3,2,1,0:T(8,128)S(1)} copy-done((f32[4,8,56,896]{3,2,1,0:T(8,128)S(1)}, f32[4,8,56,896]{3,2,1,0:T(8,128)}, u32[]{:S(2)}) %copy-start) | copy-done | bytes 6422552
  174.9 0.9 copy-done.1
  175.8 12.3 %bitcast_subtract_fusion = f32[896,1792]{1,0:T(8,128)} fusion(f32[16,56,1792]{2,1,0:T(8,128)S(1)} %broadcast_select_fusion, f32[896,896]{1,0:T(8,128)S(1)} %copy-done.1, f32[1792,896]{1,0:T(8,128)S(1)} %bitcast.6), kind=kOutput, calls=%fused_computation | convolution fusion | flops 8633483264 | bytes 22478848 | tf_op jit(solution)/shard_map/dot_general | solution.py:20
Async XLA Ops:
  172.0 2.8 %copy-start = (f32[4,8,56,896]{3,2,1,0:T(8,128)S(1)}, f32[4,8,56,896]{3,2,1,0:T(8,128)}, u32[]{:S(2)}) copy-start(f32[4,8,56,896]{3,2,1,0:T(8,128)} %get-tuple-element.16) | copy-start | bytes 19267588
  172.0 3.8 %copy-start.1 = (f32[896,896]{1,0:T(8,128)S(1)}, f32[896,896]{1,0:T(8,128)}, u32[]{:S(2)}) copy-start(f32[896,896]{1,0:T(8,128)} %get-tuple-element.15) | copy-start | bytes 9633796
where the time goes:
time: 188 us
  Pallas kernels  172 us (91%)
  matrix products  12.3 us (7%)
  local copies, waits for them, and re-layouts  3.23 us (2%)
    pallas_call x1, Pallas kernels, merge(): pl.pallas_call(kernel, out_shape=[jax.ShapeDtypeStruct((slots * nodes, 2...  167 us
    dot_general x1, matrix products, dot_nt(): lax.dot_general(left, right, (((1,), (1,)), ((), ())), precision=precisio...  12.3 us
    pallas_call x1, Pallas kernels, pick_faces(): pl.pallas_call(pick_kernel, out_shape=[jax.ShapeDtypeStruct((3, nodes, si...  4.83 us

commit v1 on v0

--- a/solution.py
+++ b/solution.py
@@ -156,7 +156,7 @@
     work_ref,
     middle_ref,
     tall_ref,
-    relay_ref,
+    flip_ref,
     z_sems,
     part_sems,
     far_sems,
@@ -165,8 +165,9 @@
     twin_sems,
     tall_sems,
     exact_sems,
-    relay_sems,
     swap_sems,
+    pass_sems,
+    flip_sems,
     local_sems,
 ):
     size = shared_ref.shape[-1]
@@ -174,7 +175,7 @@
     boxes = beta_ref.shape[0]
     slots = tall_ref.shape[0]
     wide_cols, wide_rows = cross_sems.shape[2] + 1, cross_sems.shape[3] + 1
-    relays = wide_cols == 2 and wide_rows == 2 and tiles == 2 * boxes
+    paired = wide_cols == 2 and wide_rows == 2 and tiles == 2 * boxes
     box_id = lax.axis_index("box")
     tile_id = lax.axis_index("tile")
     core = tile_id % 2
@@ -264,11 +265,37 @@
 
     def part_start(kind, pair):
         def one(i):
-            @pl.when((tile_id + i) % 2 == pair)
+            @pl.when(jnp.logical_and((tile_id + i) % 2 == pair, part_direct(kind, i)))
             def _():
                 part_copy(kind, i, tile_id).start()
 
         each(1, tiles, one)
+
+    def part_direct(kind, i):
+        if kind == 0 or not paired:
+            return tile_id >= 0
+        other = (tile_id + i) % tiles // 2
+        return jnp.logical_or(other // wide_cols == row, other % wide_cols == col)
+
+    def part_origins():
+        return ((tile_at(0, 1, 0), tile_at(1, 0)), (tile_at(1, 0, 1), tile_at(0, 1)))
+
+    def part_relay(kind, starting):
+        for way, (origin, dest) in enumerate(part_origins()):
+            ref = both_ref.at[origin] if kind == 1 else part_ref.at[1, origin]
+            copy = pltpu.make_async_remote_copy(
+                src_ref=ref,
+                dst_ref=ref,
+                send_sem=pass_sems.at[kind - 1, way],
+                recv_sem=part_sems.at[1, kind, (dest - origin + tiles) % tiles - 1],
+                device_id={"box": box_id, "tile": dest},
+                device_id_type=MESH,
+            )
+            if starting:
+                part_copy(kind, (tile_id - origin + tiles) % tiles, origin).wait_recv()
+                copy.start()
+            else:
+                copy.wait_send()
 
     def pack(pair):
         pack_ref[pair, :, :size] = beta_ref[2 * pair]
@@ -325,9 +352,6 @@
         source = rows_ref if isinstance(i, int) and isinstance(j, int) else wide_ref.at[:, sender]
         return remote(source, wide_ref.at[:, sender], twin_sems, (i, j), box_id, twin)
 
-    each(1, wide_cols, lambda i: line_copy(0, i, tile_id).start())
-    each(1, wide_rows, lambda j: line_copy(1, j, tile_id).start())
-    twin_copy(0, 0, core).start()
     keep = pltpu.make_async_copy(rows_ref, wide_ref.at[:, tile_id], local_sems.at[0])
     keep.start()
 
@@ -335,75 +359,36 @@
         flat = (box * 4 + face) * tiles + tile
         return flat // slots, flat % slots
 
+    def trim(ref, face):
+        if paired and face >= 2:
+            return ref.at[:, pl.ds(2 * size, 2 * size)]
+        return ref
+
+    def exact_copy(source, slot, dest, send_sem, face):
+        return pltpu.make_async_remote_copy(
+            src_ref=trim(source, face),
+            dst_ref=trim(exact_ref.at[slot], face),
+            send_sem=send_sem,
+            recv_sem=exact_sems.at[1, slot],
+            device_id={"box": box_id, "tile": dest},
+            device_id_type=MESH,
+        )
+
+    def exact_local(face):
+        slot = owner(box_id, face, tile_id)[1]
+        return pltpu.make_async_copy(
+            trim(own_ref.at[face], face), trim(exact_ref.at[slot], face), local_sems.at[1 + face]
+        )
+
     def exact_move(face, remote_action, local_action):
         dest, slot = owner(box_id, face, tile_id)
-        direct = dest != tile_id
-
         @pl.when(dest == tile_id)
         def _():
-            local_action(
-                pltpu.make_async_copy(own_ref.at[face], exact_ref.at[slot], local_sems.at[1 + face])
-            )
-
-        if relays:
-            dest_row, dest_col = dest // 2 // wide_cols, dest // 2 % wide_cols
-            corner = jnp.logical_and(dest_row != row, dest_col != col)
-            direct = jnp.logical_and(direct, jnp.logical_not(corner))
-            via = tile_at(0, 1) if face % 2 == 0 else tile_at(1, 0)
-
-            @pl.when(corner)
-            def _():
-                remote_action(
-                    pltpu.make_async_remote_copy(
-                        src_ref=own_ref.at[face],
-                        dst_ref=relay_ref.at[face // 2],
-                        send_sem=exact_sems.at[0, face],
-                        recv_sem=relay_sems.at[1, face // 2],
-                        device_id={"box": box_id, "tile": via},
-                        device_id_type=MESH,
-                    )
-                )
-
-        @pl.when(direct)
-        def _():
-            remote_action(
-                pltpu.make_async_remote_copy(
-                    src_ref=own_ref.at[face],
-                    dst_ref=exact_ref.at[slot],
-                    send_sem=exact_sems.at[0, face],
-                    recv_sem=exact_sems.at[1, slot],
-                    device_id={"box": box_id, "tile": dest},
-                    device_id_type=MESH,
-                )
-            )
-
-    def relay_move(half, starting):
-        dest_chip = owner(box_id, 0, 0)[0] // 2
-        dest_row, dest_col = dest_chip // wide_cols, dest_chip % wide_cols
-
-        def one(face, origin):
-            dest, slot = owner(box_id, face, origin)
-            copy = pltpu.make_async_remote_copy(
-                src_ref=relay_ref.at[half],
-                dst_ref=exact_ref.at[slot],
-                send_sem=relay_sems.at[0, half],
-                recv_sem=exact_sems.at[1, slot],
-                device_id={"box": box_id, "tile": dest},
-                device_id_type=MESH,
-            )
-            if starting:
-                remote(own_ref.at[face], relay_ref.at[half], relay_sems, (half,), box_id, origin).wait_recv()
-                copy.start()
-            else:
-                copy.wait_send()
-
-        @pl.when(jnp.logical_and(col == dest_col, row != dest_row))
-        def _():
-            one(2 * half, tile_at(0, 1))
-
-        @pl.when(jnp.logical_and(row == dest_row, col != dest_col))
-        def _():
-            one(2 * half + 1, tile_at(1, 0))
+            local_action(exact_local(face))
+
+        @pl.when(dest != tile_id)
+        def _():
+            remote_action(exact_copy(own_ref.at[face], slot, dest, exact_sems.at[0, face], face))
 
     def tall_move(box, face, starting):
         dest, slot = owner(box, face, tile_id)
@@ -428,9 +413,6 @@
             else:
                 copy.wait_send()
 
-    for face in range(4):
-        exact_move(face, start, start)
-
     def spread(step, starting):
         for origin in (box_id - step, box_id + step):
 
@@ -443,8 +425,6 @@
         far_step(step, False, came)
         if step < boxes - 1:
             far_step(step + 1, True, start)
-
-        spread(step, True)
 
     def forward_row(i):
         line_copy(0, i, line_source(0, i)).wait_recv()
@@ -469,13 +449,19 @@
         each(1, wide_cols, forward_row)
         each(1, wide_rows, forward_col)
 
-    def forward_relay():
-        if relays:
-            for half in range(2):
-                relay_move(half, True)
-
     def part_wait(kind):
-        each(1, tiles, lambda i: part_copy(kind, i, (tile_id + tiles - i) % tiles).wait_recv())
+        def one(i):
+            origin = (tile_id + tiles - i) % tiles
+            fresh = tile_id >= 0
+            if kind > 0 and paired:
+                for early, _ in part_origins():
+                    fresh = jnp.logical_and(fresh, origin != early)
+
+            @pl.when(fresh)
+            def _():
+                part_copy(kind, i, origin).wait_recv()
+
+        each(1, tiles, one)
 
     def matrix(ref, span):
         if nodes % 8 == 0:
@@ -490,13 +476,32 @@
     def half_swap(index):
         return remote(half_ref.at[index], other_ref.at[index], swap_sems, (2 + index,), box_id, twin)
 
+    def part_forward(kind):
+        if paired:
+            part_relay(kind, True)
+
+    def line_start():
+        part_forward(2)
+        each(1, wide_cols, lambda i: line_copy(0, i, tile_id).start())
+        each(1, wide_rows, lambda j: line_copy(1, j, tile_id).start())
+        twin_copy(0, 0, core).start()
+
+    def exact_start():
+        for face in range(4):
+            exact_move(face, start, start)
+
     hooks = {
-        (1, 0): lambda: forward_far(1),
-        (1, 2): forward_line,
-        (1, 5): lambda: forward_far(2),
-        (2, 0): forward_cross,
-        (2, 2): forward_relay,
-        (2, 4): lambda: forward_far(3),
+        (0, 2): lambda: part_forward(1),
+        (0, 4): line_start,
+        (0, 6): lambda: forward_far(1),
+        (1, 0): forward_line,
+        (1, 2): lambda: forward_far(2),
+        (1, 3): lambda: spread(2, True),
+        (1, 4): forward_cross,
+        (1, 5): lambda: spread(1, True),
+        (1, 6): exact_start,
+        (2, 0): lambda: forward_far(3),
+        (2, 1): lambda: spread(3, True),
     }
 
     def stage(index, carry):
@@ -618,20 +623,46 @@
             left_ref[slot * nodes : (slot + 1) * nodes, :] = tall_ref[slot]
         left_ref[...] = dot(left_ref[...], middle_ref[...], HIGH)
 
-    def exact_wait(slot):
+    def flip_copy(slot):
+        half = exact_ref.at[slot, :, pl.ds(2 * size, 2 * size)]
+        return remote(half, flip_ref.at[slot], flip_sems, (slot,), box_id, twin)
+
+    def exact_wait(slot, upper):
         source = (tile_id * slots + slot) % tiles
-
-        @pl.when(jnp.logical_and(source != tile_id, row_box == box_id))
-        def _():
-            remote(own_ref.at[0], exact_ref.at[slot], exact_sems, (slot,), box_id, twin).wait_recv()
-
-    each(0, slots, exact_wait)
+        face = 0 if upper else 2
+
+        @pl.when(source != tile_id)
+        def _():
+            exact_copy(own_ref.at[0], slot, twin, exact_sems.at[0, 0], face).wait_recv()
+            if upper and paired:
+                flip_copy(slot).start()
 
     for face in range(4):
         exact_move(face, sent, lambda copy: copy.wait())
-    if relays:
-        for half in range(2):
-            relay_move(half, False)
+    if paired:
+
+        @pl.when(jnp.logical_and(row_box == box_id, core == 0))
+        def _():
+            for slot in (tile_id, tile_id + tiles):
+                flip_copy(slot).start()
+            each(0, slots, lambda slot: exact_wait(slot, True))
+            each(0, slots, lambda slot: flip_copy(slot).wait_send())
+
+        @pl.when(jnp.logical_and(row_box == box_id, core == 1))
+        def _():
+            each(0, slots, lambda slot: exact_wait(slot, False))
+            each(0, slots, lambda slot: flip_copy(slot).wait_recv())
+            tall_ref[...] = flip_ref[...].reshape(slots * nodes, 2 * size).T.reshape(slots, nodes, 2 * size)
+            mirror = pltpu.make_async_copy(tall_ref, exact_ref.at[:, :, pl.ds(0, 2 * size)], local_sems.at[0])
+            mirror.start()
+            mirror.wait()
+
+    else:
+
+        @pl.when(row_box == box_id)
+        def _():
+            each(0, slots, lambda slot: exact_wait(slot, True))
+
     for step in range(1, boxes):
         far_step(step, True, sent)
         link_step(step, True, sent)
@@ -640,8 +671,15 @@
     across_copy(own_pair).wait_send()
     side_copy().wait_send()
     back_copy(own_side).wait_send()
+    def part_sent(kind, i):
+        @pl.when(part_direct(kind, i))
+        def _():
+            part_copy(kind, i, tile_id).wait_send()
+
     for kind in range(3):
-        each(1, tiles, lambda i: part_copy(kind, i, tile_id).wait_send())
+        each(1, tiles, lambda i: part_sent(kind, i))
+        if kind > 0 and paired:
+            part_relay(kind, False)
     each(1, wide_cols, lambda i: line_copy(0, i, tile_id).wait_send())
     each(1, wide_rows, lambda j: line_copy(1, j, tile_id).wait_send())
 
@@ -701,7 +739,7 @@
             vmem(BLOCK, 2 * BLOCK),
             vmem(2 * size, 2 * size),
             vmem(slots, nodes, 2 * size),
-            vmem(2, nodes, 4 * size),
+            vmem(slots, nodes, 2 * size),
             sems(4, boxes - 1),
             sems(3, tiles - 1),
             sems(2, boxes - 1),
@@ -710,8 +748,9 @@
             sems(wide_cols, wide_rows),
             sems(slots),
             sems(slots),
-            sems(2),
             sems(5),
+            pltpu.SemaphoreType.DMA((2, 2)),
+            sems(slots),
             pltpu.SemaphoreType.DMA((5 + slots,)),
         ],
         compiler_params=pltpu.CompilerParams(

time: 188 us -> 171 us (0.910)
  the two profiles are of different devices: /device:TPU:7 before, /device:TPU:11 now
where the time goes in v1:
time: 171 us
  Pallas kernels  153 us (89%)
  matrix products  12.3 us (7%)
  other arithmetic  3.47 us (2%)
  local copies, waits for them, and re-layouts  2.11 us (1%)
    pallas_call x1, Pallas kernels, merge(): pl.pallas_call(kernel, out_shape=[jax.ShapeDtypeStruct((slots * nodes, 2...  148 us
    dot_general x1, matrix products, dot_nt(): lax.dot_general(left, right, (((1,), (1,)), ((), ())), precision=precisio...  12.3 us
    pallas_call x1, Pallas kernels, pick_faces(): pl.pallas_call(pick_kernel, out_shape=[jax.ShapeDtypeStruct((3, nodes, si...  4.84 us
    select_n x1, other arithmetic, per_device(): exact = jnp.where(same, exact.reshape(left.shape[0], 4 * size), 0.0)  3.47 us

profile of v1, /device:TPU:11, one launch (start us, length us, event | category | flops | bytes accessed | tf_op | source)
XLA Modules:
  0.0 170.9 jit_solution(12753732729746164419)
XLA Ops:
  0.0 4.8 %pick_faces.1 = (f32[3,56,448]{2,1,0:T(8,128)}, f32[4,56,896]{2,1,0:T(8,128)}, f32[4,56,1792]{2,1,0:T(8,128)}) custom-call(s32[4,6]{1,0:T(4,128)} %slots_ref.1, f32[6,56,2688]{2,1,0:T(8,128)} %bitcast.7), custom_call_target="tpu_custom_call" | custom-call | tf_op jit(solution)/shard_map/pick_faces/pallas_call | solution.py:55
  4.8 148.2 %merge.1 = (f32[896,896]{1,0:T(8,128)}, f32[4,8,56,896]{3,2,1,0:T(8,128)}, f32[16,56,1792]{2,1,0:T(8,128)}) custom-call(f32[3,56,448]{2,1,0:T(8,128)} %get-tuple-element.11.refs_0_, f32[4,56,896]{2,1,0:T(8,128)} %get-tuple-element.12.refs_1_, f32[4,56,1792]{2,1,0:T(8,128)} %get-tuple-element.13.refs_2_), custom_call_target="tpu_custom_call" | custom-call | tf_op jit(solution)/shard_map/merge/pallas_call | solution.py:715
  153.1 0.0 copy-start
  153.1 0.0 copy-start.1
  153.1 3.5 %broadcast_select_fusion = f32[16,56,1792]{2,1,0:T(8,128)S(1)} fusion(f32[16,56,1792]{2,1,0:T(8,128)} %get-tuple-element.14, pred[]{:T(512)S(6)} %eq.3), kind=kLoop, calls=%fused_computation.1 | loop fusion | flops 1605632 | bytes 12845057 | tf_op jit(solution)/shard_map/jit(_where)/select_n | solution.py:770
  156.6 1.2 copy-done
  157.8 0.9 copy-done.1
  158.7 12.3 %bitcast_subtract_fusion = f32[896,1792]{1,0:T(8,128)} fusion(f32[16,56,1792]{2,1,0:T(8,128)S(1)} %broadcast_select_fusion, f32[896,896]{1,0:T(8,128)S(1)} %copy-done.1, f32[1792,896]{1,0:T(8,128)S(1)} %bitcast.6), kind=kOutput, calls=%fused_computation | convolution fusion | flops 8633483264 | bytes 22478848 | tf_op jit(solution)/shard_map/dot_general | solution.py:20
Async XLA Ops:
  153.1 4.7 %copy-start = (f32[4,8,56,896]{3,2,1,0:T(8,128)S(1)}, f32[4,8,56,896]{3,2,1,0:T(8,128)}, u32[]{:S(2)}) copy-start(f32[4,8,56,896]{3,2,1,0:T(8,128)} %get-tuple-element.16) | copy-start | bytes 19267588
  153.1 5.6 %copy-start.1 = (f32[896,896]{1,0:T(8,128)S(1)}, f32[896,896]{1,0:T(8,128)}, u32[]{:S(2)}) copy-start(f32[896,896]{1,0:T(8,128)} %get-tuple-element.15) | copy-start | bytes 9633796

commit v2 on v1

--- a/solution.py
+++ b/solution.py
@@ -496,10 +496,10 @@
         (0, 6): lambda: forward_far(1),
         (1, 0): forward_line,
         (1, 2): lambda: forward_far(2),
-        (1, 3): lambda: spread(2, True),
-        (1, 4): forward_cross,
+        (1, 3): forward_cross,
+        (1, 4): exact_start,
         (1, 5): lambda: spread(1, True),
-        (1, 6): exact_start,
+        (1, 6): lambda: spread(2, True),
         (2, 0): lambda: forward_far(3),
         (2, 1): lambda: spread(3, True),
     }
@@ -767,8 +767,9 @@
     tiles, boxes = lax.axis_size("tile"), lax.axis_size("box")
     box_id, tile_id = lax.axis_index("box"), lax.axis_index("tile")
     same = tile_id * boxes // tiles == box_id
-    exact = jnp.where(same, exact.reshape(left.shape[0], 4 * size), 0.0)
-    return exact - dot_nt(left, wide.reshape(4 * tiles * nodes, 2 * size), HIGH)
+    exact = exact.reshape(left.shape[0], 4 * size)
+    change = dot_nt(left, wide.reshape(4 * tiles * nodes, 2 * size), HIGH)
+    return jnp.where(same, exact - change, -change)
 
 
 def solution(mesh):

time: 171 us -> 162 us (0.947)
  the two profiles are of different devices: /device:TPU:11 before, /device:TPU:7 now
where the time goes in v2:
time: 162 us; the launch traced here: 160 us
  Pallas kernels  143 us (88%)
  matrix products  16.5 us (10%)
    pallas_call x1, Pallas kernels, merge(): pl.pallas_call(kernel, out_shape=[jax.ShapeDtypeStruct((slots * nodes, 2...  138 us
    dot_general x1, matrix products, dot_nt(): lax.dot_general(left, right, (((1,), (1,)), ((), ())), precision=precisio...  16.5 us
    pallas_call x1, Pallas kernels, pick_faces(): pl.pallas_call(pick_kernel, out_shape=[jax.ShapeDtypeStruct((3, nodes, si...  4.83 us

profile of v2, /device:TPU:7, one launch (start us, length us, event | category | flops | bytes accessed | tf_op | source)
XLA Modules:
  0.0 159.6 jit_solution(11227463106761661978)
XLA Ops:
  0.0 4.8 %pick_faces.1 = (f32[3,56,448]{2,1,0:T(8,128)}, f32[4,56,896]{2,1,0:T(8,128)}, f32[4,56,1792]{2,1,0:T(8,128)}) custom-call(s32[4,6]{1,0:T(4,128)} %slots_ref.1, f32[6,56,2688]{2,1,0:T(8,128)} %bitcast.9), custom_call_target="tpu_custom_call" | custom-call | tf_op jit(solution)/shard_map/pick_faces/pallas_call | solution.py:55
  4.8 138.2 %merge.1 = (f32[896,896]{1,0:T(8,128)}, f32[4,8,56,896]{3,2,1,0:T(8,128)}, f32[16,56,1792]{2,1,0:T(8,128)}) custom-call(f32[3,56,448]{2,1,0:T(8,128)} %get-tuple-element.11.refs_0_, f32[4,56,896]{2,1,0:T(8,128)} %get-tuple-element.12.refs_1_, f32[4,56,1792]{2,1,0:T(8,128)} %get-tuple-element.13.refs_2_), custom_call_target="tpu_custom_call" | custom-call | tf_op jit(solution)/shard_map/merge/pallas_call | solution.py:715
  143.0 16.5 %fusion = f32[896,1792]{1,0:T(8,128)} fusion(f32[16,56,1792]{2,1,0:T(8,128)} %get-tuple-element.14, pred[]{:T(512)S(6)} %eq.3, f32[896,896]{1,0:T(8,128)} %get-tuple-element.15, f32[1792,896]{1,0:T(8,128)} %bitcast.8), kind=kOutput, calls=%fused_computation.1 | convolution fusion | flops 8636694528 | bytes 22478848 | tf_op jit(solution)/shard_map/dot_general | solution.py:20
